TPU v7x, 512 devices: a whole 4x8x8 slice. The times are simulated.
512 devices in a mesh: dp: 256 (over x, y, z), outer: 2 (over core).
Axes of the slice: x: 4, y: 8, z: 8, core: 2. Of those that a mesh axis runs over, the one named last changes fastest.
Arguments:
- gradient: float32 [512, 131072], P(('dp', 'outer')), may hold values from -6 to 6
- residual: float32 [512, 131072], P(('dp', 'outer')), may hold values from -6 to 6
- indices: int32 [512, 512], P(('dp', 'outer')), may hold values from 0 to 131071, as said below
- params: float32 [131072], replicated, may hold values from -6 to 6
Outputs:
- new_params: float32 [131072], replicated
- new_residual: float32 [512, 131072], P(('dp', 'outer'))
Inputs may be any that keep to these rules, and one draw needn't show every extreme that they name: Within each worker's row the 512 indices are distinct and increasing: index j lies in [j * 256, (j + 1) * 256). Different workers often pick the same coordinate.
All inputs are finite; a program needn't handle non-finite values.
Results may differ from a plain program's by a relative error of at most 0.0003.
Values sent between devices are 32-bit elements.
No kernel may reach another device: no remote copies, remote signals or barrier semaphores. Data moves between devices by JAX's collectives and lax.ppermute only.
A program may use at most 64 MiB of HBM per device.

v0:
```python
import jax
import jax.numpy as jnp
from jax import lax
from jax.sharding import Mesh
from jax.sharding import PartitionSpec as P

DP_OUTER = ("dp_0", "dp_1", "dp_2", "outer")
step_size = 0.5


def split_up(array, dim, devices):
    return jnp.stack(jnp.split(array, devices, axis=dim))


def scatter_pairs(array, chips, core, dim):
    sizes = (lax.axis_size(chips), lax.axis_size(core))
    parts = split_up(array, dim, sizes[0] * sizes[1])
    inside = parts.shape[1:]
    parts = parts.reshape(*sizes, *inside).swapaxes(0, 1).reshape(-1, *inside)
    parts = lax.psum_scatter(parts, core, scatter_dimension=0, tiled=True)
    return lax.psum_scatter(parts, chips, scatter_dimension=0, tiled=True)[0]


def shards(gradient, residual, indices, params):
    accumulated = gradient[0] + residual[0]
    positions = indices[0]
    values_sent = accumulated[positions]
    new_residual = accumulated.at[positions].set(jnp.float32(0.0))[None, :]
    empty = jnp.zeros((accumulated.shape[0],), jnp.float32)
    spread = empty.at[positions].add(values_sent)
    portion = scatter_pairs(spread, ("dp_0", "dp_1", "dp_2"), "outer", 0)
    length = portion.shape[0]
    first = lax.axis_index(DP_OUTER) * length
    own_params = lax.dynamic_slice_in_dim(params, first, length)
    updated = own_params - step_size * portion
    new_params = lax.all_gather(updated, DP_OUTER, axis=0, tiled=True)
    return (new_params, new_residual)


def solution(mesh):
    torus = Mesh(
        mesh.devices.reshape(4, 8, 8, mesh.shape["outer"]), ("dp_0", "dp_1", "dp_2", "outer")
    )
    placed = (P(DP_OUTER, None), P(DP_OUTER, None), P(DP_OUTER, None), P())
    return jax.shard_map(
        shards, mesh=torus, in_specs=placed, out_specs=(P(), P(DP_OUTER, None)), check_vma=False
    )
```

profile of v0, /device:TPU:1, one launch (start us, length us, event | category | flops | bytes accessed | tf_op | source)
XLA Modules:
  0.0 359.0 jit_solution(5409333906929286416)
XLA Ops:
  7.2 0.0 reduce-scatter.2.cloned.1.call-start
  7.2 0.7 compare_select_fusion
  7.9 1.7 add.41
  9.7 3.1 gather_fusion
  12.8 3.7 %scatter_custom_fusion = f32[131072]{0:T(1024)S(1)} fusion(s32[512]{0:T(512)S(1)} %bitcast.530, f32[512]{0:T(512)S(1)} %gather_fusion, f32[]{:T(128)} %constant.34.clone.1), kind=kCustom, calls=%fused_computation.4 | custom fusion | flops 512 | bytes 524292 | tf_op jit(solution)/shard_map/scatter-add | solution.py:30
  17.0 0.8 concatenate
  17.9 0.8 concatenate.1
  18.7 0.3 reshape.41
  19.0 0.8 copy.7
  19.9 0.0 reduce-scatter.2.cloned.1.call-update
  19.9 0.0 all-reduce.3.cloned.1.call-start
  19.9 23.1 %reduce-scatter.2.cloned.1.call-done = f32[256,256]{1,0:T(8,128)} async-done(((f32[512,256]{1,0:T(8,128)}), f32[256,256]{1,0:T(8,128)}) %reduce-scatter.2.cloned.1.call-update) | async-done | bytes 262160 | tf_op jit(solution)/shard_map/reduce_scatter | solution.py:20
  43.0 0.0 all-reduce.3.cloned.1.call-update
  43.1 2.7 scatter_fusion
  45.8 0.0 copy-start
  45.8 1.3 dynamic-slice
  47.1 230.3 %all-reduce.3.cloned.1.call-done = f32[256,256]{1,0:T(8,128)} async-done(((f32[256,256]{1,0:T(8,128)}), f32[256,256]{1,0:T(8,128)}) %all-reduce.3.cloned.1.call-update) | async-done | bytes 262160
  277.4 1.3 dynamic-slice_multiply_fusion
  278.8 0.8 dynamic-slice_subtract_fusion
  279.6 71.8 %all-gather = f32[512,1,256]{2,1,0:T(1,128)S(1)} all-gather(f32[1,1,256]{2,1,0:T(1,128)S(1)} %bitcast.1044), channel_id=1, replica_groups=mesh['dp_0'=4,'dp_1'=8,'dp_2'=8,'outer'=2] {'dp_0','dp_1','dp_2','outer'}, dimensions={0}, use_global_device_ids=true | all-gather | bytes 525312 | tf_op jit(solution)/shard_map/all_gather | solution.py:36
  351.4 0.8 copy.11
  352.2 0.0 copy-done
  (31 shorter events, 0.4 us)
Async XLA Ops:
  7.2 35.9 %reduce-scatter.2.cloned.1.call-start = ((), (), s32[]{:S(2)}) async-start(), calls=%async_computation.1 | async-start | bytes 786432 | tf_op jit(solution)/shard_map/reduce_scatter | solution.py:20
  19.9 257.5 %all-reduce.3.cloned.1.call-start = ((), (), s32[]{:S(2)}) async-start(), calls=%async_computation.2 | async-start | bytes 524288
  45.8 306.4 %copy-start = (f32[131072]{0:T(1024)}, f32[131072]{0:T(1024)S(1)}, u32[]{:S(2)}) copy-start(f32[131072]{0:T(1024)S(1)} %scatter_fusion) | copy-start | bytes 1572868
Sparse Core Ops, SparseCore 0:
  20.0 22.9 reduce-scatter.1
  48.0 229.4 all-reduce.2
where the time goes:
time: 359 us
  waiting for transfers between devices  253 us (70%)
  blocking collectives  71.8 us (20%)
  between operations  14.3 us (4%)
  local copies, waits for them, and re-layouts  11.1 us (3%)
  other arithmetic  8.24 us (2%)
    unnamed x3, waiting for transfers between devices  230 us
    all_gather x1, blocking collectives, shards(): new_params = lax.all_gather(updated, DP_OUTER, axis=0, tiled=True)  71.8 us
    reduce_scatter x1, waiting for transfers between devices, scatter_pairs(): parts = lax.psum_scatter(parts, core, scatter_dimension=0, tiled=True)  23.1 us
  transfers between devices with their start and end apart: 2, of which 2 were waited for; matrix products, arithmetic and copies ran while one was open for 1% of the time, Pallas kernels for 0%

commit v1 on v0

--- a/solution.py
+++ b/solution.py
@@ -33,7 +33,9 @@
     first = lax.axis_index(DP_OUTER) * length
     own_params = lax.dynamic_slice_in_dim(params, first, length)
     updated = own_params - step_size * portion
-    new_params = lax.all_gather(updated, DP_OUTER, axis=0, tiled=True)
+    new_params = jnp.concatenate(
+        lax.all_to_all(jnp.stack([updated] * lax.axis_size(DP_OUTER)), DP_OUTER, 0, 0), axis=0
+    )
     return (new_params, new_residual)
 
 

time: 359 us -> 327 us (0.911)
  blocking collectives: 71.8 us -> 0 us
  waiting for transfers between devices: 253 us -> 275 us
  starting transfers between devices: 0.08 us -> 17.1 us
    all_gather x1 -> x0, blocking collectives: 71.8 us -> none  [shards(): new_params = lax.all_gather(updated, DP_OUTER, axis=0, tiled=True)]
    all_to_all x0 -> x1, waiting for transfers between devices: none -> 19.1 us  [shards(): lax.all_to_all(jnp.stack([updated] * lax.axis_size(DP_OUTER)), DP_OUTER,...]
    all_to_all x0 -> x1, starting transfers between devices: none -> 17.1 us  [shards(): lax.all_to_all(jnp.stack([updated] * lax.axis_size(DP_OUTER)), DP_OUTER,...]
  transfers between devices with their start and end apart: 2 -> 3, of which waited for: 2 -> 3; matrix products, arithmetic and copies ran while one was open for 1% -> 1% of each run, Pallas kernels for 0% -> 0%
where the time goes in v1:
time: 327 us
  waiting for transfers between devices  275 us (84%)
  starting transfers between devices  17.1 us (5%)
  between operations  14.3 us (4%)
  local copies, waits for them, and re-layouts  12.1 us (4%)
  other arithmetic  8.24 us (3%)
    unnamed x3, waiting for transfers between devices  233 us
    reduce_scatter x1, waiting for transfers between devices, scatter_pairs(): parts = lax.psum_scatter(parts, core, scatter_dimension=0, tiled=True)  23.1 us
    all_to_all x1, waiting for transfers between devices, shards(): lax.all_to_all(jnp.stack([updated] * lax.axis_size(DP_OUTER)), DP_OUTER,...  19.1 us
    all_to_all x1, starting transfers between devices, shards(): lax.all_to_all(jnp.stack([updated] * lax.axis_size(DP_OUTER)), DP_OUTER,...  17.1 us
  transfers between devices with their start and end apart: 3, of which 3 were waited for; matrix products, arithmetic and copies ran while one was open for 1% of the time, Pallas kernels for 0%

profile of v1, /device:TPU:1, one launch (start us, length us, event | category | flops | bytes accessed | tf_op | source)
XLA Modules:
  0.0 327.2 jit_solution(6292188392576828960)
XLA Ops:
  7.2 0.0 reduce-scatter.2.cloned.1.call-start
  7.2 0.7 compare_select_fusion
  7.9 1.7 add.41
  9.7 3.1 gather_fusion
  12.8 3.7 %scatter_custom_fusion = f32[131072]{0:T(1024)S(1)} fusion(s32[512]{0:T(512)S(1)} %bitcast.529, f32[512]{0:T(512)S(1)} %gather_fusion, f32[]{:T(128)} %constant.34.clone.1), kind=kCustom, calls=%fused_computation.4 | custom fusion | flops 512 | bytes 524292 | tf_op jit(solution)/shard_map/scatter-add | solution.py:30
  17.0 0.8 concatenate
  17.9 0.8 concatenate.1
  18.7 0.3 reshape.52
  19.0 0.8 copy.7
  19.9 0.0 reduce-scatter.2.cloned.1.call-update
  19.9 0.0 all-reduce.3.cloned.1.call-start
  19.9 23.1 %reduce-scatter.2.cloned.1.call-done = f32[256,256]{1,0:T(8,128)} async-done(((f32[512,256]{1,0:T(8,128)}), f32[256,256]{1,0:T(8,128)}) %reduce-scatter.2.cloned.1.call-update) | async-done | bytes 262160 | tf_op jit(solution)/shard_map/reduce_scatter | solution.py:20
  43.0 0.0 all-reduce.3.cloned.1.call-update
  43.1 1.3 dynamic-slice
  44.3 233.1 %all-reduce.3.cloned.1.call-done = f32[256,256]{1,0:T(8,128)} async-done(((f32[256,256]{1,0:T(8,128)}), f32[256,256]{1,0:T(8,128)}) %all-reduce.3.cloned.1.call-update) | async-done | bytes 262160
  277.4 1.3 dynamic-slice_multiply_fusion
  278.8 0.8 dynamic-slice_subtract_fusion
  279.6 1.1 stack.2567
  280.6 17.1 %all-to-all-start = ((f32[512,1,256]{2,1,0:T(1,128)}), f32[512,1,256]{2,1,0:T(1,128)S(1)}, u32[]{:S(2)}, u32[]{:S(2)}) async-start(f32[512,1,256]{2,1,0:T(1,128)} %stack.2567), calls=%async_computation.1 | async-start | bytes 1048576 | tf_op jit(solution)/shard_map/all_to_all | solution.py:37
  297.7 2.7 scatter_fusion
  300.4 0.0 copy-start
  300.4 19.1 %all-to-all-done = f32[512,1,256]{2,1,0:T(1,128)S(1)} async-done(((f32[512,1,256]{2,1,0:T(1,128)}), f32[512,1,256]{2,1,0:T(1,128)S(1)}, u32[]{:S(2)}, u32[]{:S(2)}) %all-to-all-start) | async-done | bytes 524320 | tf_op jit(solution)/shard_map/all_to_all | solution.py:37
  319.5 0.8 copy.11
  320.4 0.0 copy-done
  (31 shorter events, 0.4 us)
Async XLA Ops:
  7.2 35.9 %reduce-scatter.2.cloned.1.call-start = ((), (), s32[]{:S(2)}) async-start(), calls=%async_computation.2 | async-start | bytes 786432 | tf_op jit(solution)/shard_map/reduce_scatter | solution.py:20
  19.9 257.5 %all-reduce.3.cloned.1.call-start = ((), (), s32[]{:S(2)}) async-start(), calls=%async_computation.3 | async-start | bytes 524288
  280.6 38.9 %all-to-all-start = ((f32[512,1,256]{2,1,0:T(1,128)}), f32[512,1,256]{2,1,0:T(1,128)S(1)}, u32[]{:S(2)}, u32[]{:S(2)}) async-start(f32[512,1,256]{2,1,0:T(1,128)} %stack.2567), calls=%async_computation.1 | async-start | bytes 1048576 | tf_op jit(solution)/shard_map/all_to_all | solution.py:37
  300.4 20.0 %copy-start = (f32[131072]{0:T(1024)}, f32[131072]{0:T(1024)S(1)}, u32[]{:S(2)}) copy-start(f32[131072]{0:T(1024)S(1)} %scatter_fusion) | copy-start | bytes 1572868
Sparse Core Ops, SparseCore 0:
  20.0 22.9 reduce-scatter.1
  48.0 229.4 all-reduce.2
